TPU v7x, 32 devices: a whole 2x2x4 slice. The times are simulated.
32 devices in a mesh: wa: 16 (over z, y, core), ha: 2 (over x).
Axes of the slice: x: 2, y: 2, z: 4, core: 2. Of those that a mesh axis runs over, the one named last changes fastest.
Arguments:
- tokens: bfloat16 [16384, 4096], P('wa'), may hold values from -6 to 6
- expert_ids: int32 [16384, 8], P('wa'), may hold values from 0 to 127, as said below
- keep_mask: int32 [16384, 8], P('wa'), may hold values from 0 to 1, as said below
- route_weight: float32 [16384, 8], P('wa'), may hold values from 0.2 to 1
- gate_weight: bfloat16 [4096, 1536], P('wa', 'ha'), may hold values from -0.09375 to 0.09375
- up_weight: bfloat16 [4096, 1536], P('wa', 'ha'), may hold values from -0.09375 to 0.09375
- down_weight: bfloat16 [4096, 1536], P('wa', 'ha'), may hold values from -0.15625 to 0.15625
Outputs:
- mixed: bfloat16 [16384, 4096], P('wa', 'ha')
Inputs may be any that keep to these rules, and one draw needn't show every extreme that they name: `expert_ids`: each row names 8 different experts. keep_mask[t, k] is 1 exactly where fewer than 128 earlier tokens of the same block of 1024 rows name expert_ids[t, k]; in some block 128 tokens naming expert 0 are kept.
All inputs are finite; a program needn't handle non-finite values.
Results may differ from a plain program's by a relative error of at most 0.005.
Values may be sent and summed in bfloat16 or wider, within the bound.
A program may use at most 128 MiB of HBM per device.

v0:
```python
import jax
import jax.numpy as jnp
from jax import lax
from jax.sharding import PartitionSpec as P

CAP = 128


def prefix(value, axis, join, neutral):
    count, mine = (lax.axis_size(axis), lax.axis_index(axis))
    pieces = lax.all_gather(value, axis)
    subtotal = jnp.full_like(value, 0) + jnp.asarray(neutral, value.dtype)

    def turn(position, subtotal):
        longer = join(subtotal, pieces[position])
        return jnp.where(position < mine, longer, subtotal)

    return lax.fori_loop(0, count - 1, turn, subtotal)


def add_counts(earlier, later):
    return earlier + later


def global_admit(chosen, position):
    counted = jnp.sum(chosen).reshape(1)
    earlier = prefix(counted, "wa", add_counts, jnp.zeros((1,), jnp.int32))
    capacity = lax.axis_size("wa") * CAP // 2
    return chosen * (earlier[0] + position < capacity).astype(jnp.int32)


def slot_table(position, marked):
    slot_ids = jnp.arange(CAP, dtype=jnp.int32)
    return (position[None, :] == slot_ids[:, None]) & (marked[None, :] == 1)


def run_expert(slot_rows, gate_weight, up_weight, down_weight):
    gate_next = jnp.dot(
        slot_rows,
        lax.all_gather(gate_weight, "wa", axis=0, tiled=True),
        preferred_element_type=jnp.float32,
    )
    up_next = jnp.dot(
        slot_rows,
        lax.all_gather(up_weight, "wa", axis=0, tiled=True),
        preferred_element_type=jnp.float32,
    )
    hidden = (jax.nn.silu(gate_next) * up_next).astype(jnp.bfloat16)
    return lax.dot_general(
        hidden,
        lax.all_gather(down_weight, "wa", axis=0, tiled=True),
        (((1,), (1,)), ((), ())),
        preferred_element_type=jnp.float32,
    )


def per_device(tokens, expert_ids, keep_mask, route_weight, gate_weight, up_weight, down_weight):
    matches = (expert_ids == 0) & (keep_mask == 1)
    chosen = jnp.any(matches, axis=1).astype(jnp.int32)
    route_sum = jnp.sum(jnp.where(matches, route_weight, jnp.float32(0.0)), axis=1)
    position = jnp.cumsum(chosen) - chosen
    admitted = global_admit(chosen, position)
    dispatch = slot_table(position, admitted)
    slot_rows = jnp.dot(
        dispatch.astype(jnp.bfloat16), tokens, preferred_element_type=jnp.float32
    ).astype(jnp.bfloat16)
    expert_out = run_expert(slot_rows, gate_weight, up_weight, down_weight)
    final_table = slot_table(position, admitted)
    combine_map = jnp.where(final_table.T, route_sum[:, None], jnp.float32(0.0))
    halves = lax.psum_scatter(expert_out, "ha", scatter_dimension=1, tiled=True)
    mixed = jnp.dot(
        combine_map, halves, precision=lax.Precision.HIGHEST, preferred_element_type=jnp.float32
    )
    return mixed.astype(jnp.bfloat16)


def solution(mesh):
    return jax.shard_map(
        per_device,
        mesh=mesh,
        in_specs=(
            P("wa", None),
            P("wa", None),
            P("wa", None),
            P("wa", None),
            P("wa", "ha"),
            P("wa", "ha"),
            P("wa", "ha"),
        ),
        out_specs=P("wa", "ha"),
        check_vma=False,
    )
```

profile of v0, /device:TPU:0, one launch (start us, length us, event | category | flops | bytes accessed | tf_op | source)
XLA Modules:
  0.0 254.8 jit_solution(10121087111049697661)
XLA Ops:
  6.5 0.7 all-gather.4.cloned.1.call-update
  7.3 0.7 all-gather.6.cloned.1.call-update
  8.1 0.7 all-gather.8.cloned.1.call-update
  8.8 0.8 select_reduce_fusion
  9.6 1.2 dynamic-slice
  10.9 0.7 convert_reduce_fusion
  11.6 1.3 dynamic-update-slice
  12.9 14.4 %all-reduce = s32[16]{0:T(128)S(1)} all-reduce(s32[16]{0:T(128)S(1)} %dynamic-update-slice), channel_id=1, replica_groups=mesh['wa'=16,'ha'=2] {'wa'}, use_global_device_ids=true, to_apply=%add | all-reduce | flops 16 | bytes 128
  27.6 18.4 %while.13 = (s32[]{:T(128)}, s32[1]{0:T(128)}, s32[]{:T(128)}, s32[16,1]{0,1:T(1,128)S(1)}, s32[]{:T(128)}) while((s32[]{:T(128)}, s32[1]{0:T(128)}, s32[]{:T(128)}, s32[16,1]{0,1:T(1,128)S(1)}, s32[]{:T(128)}) %tuple.41), condition=%wide.region_5.6_spmd, body=%wide.region_4.5_spmd.sunk | while | flops 5 | bytes 107 | solution.py:18
  27.6 0.6 constant_dynamic-slice_fusion.2
  28.9 0.6 constant_dynamic-slice_fusion.2
  30.1 0.6 constant_dynamic-slice_fusion.2
  31.3 0.6 constant_dynamic-slice_fusion.2
  32.6 0.6 constant_dynamic-slice_fusion.2
  33.8 0.6 constant_dynamic-slice_fusion.2
  35.0 0.6 constant_dynamic-slice_fusion.2
  36.3 0.6 constant_dynamic-slice_fusion.2
  37.5 0.6 constant_dynamic-slice_fusion.2
  38.7 0.6 constant_dynamic-slice_fusion.2
  39.9 0.6 constant_dynamic-slice_fusion.2
  41.2 0.6 constant_dynamic-slice_fusion.2
  42.4 0.6 constant_dynamic-slice_fusion.2
  43.6 0.6 constant_dynamic-slice_fusion.2
  44.9 0.6 constant_dynamic-slice_fusion.2
  46.3 4.7 %convolution_convert_fusion = bf16[128,4096]{1,0:T(8,128)(2,1)S(1)} fusion(bf16[1024,4096]{1,0:T(8,128)(2,1)} %param.9, s32[1024]{0:T(1024)S(1)} %get-tuple-element.96, pred[1024]{0:T(1024)(128)(4,1)S(1)} %get-tuple-element.95), kind=kOutput, calls=%fused_computation.1 | convolution fusion | flops 1074528256 | bytes 9442304 | tf_op jit(solution)/shard_map/dot_general | solution.py:64
  51.0 22.8 %all-gather.4.cloned.1.call-done = bf16[4096,768]{1,0:T(8,128)(2,1)} async-done(((bf16[256,768]{1,0:T(8,128)(2,1)}), bf16[4096,768]{1,0:T(8,128)(2,1)}) %all-gather.4.cloned.1.call-update) | async-done | bytes 6291472 | tf_op jit(solution)/shard_map/all_gather | solution.py:40
  73.8 3.8 %fusion.22 = f32[128,768]{1,0:T(8,128)S(1)} fusion(bf16[128,4096]{1,0:T(8,128)(2,1)S(1)} %convolution_convert_fusion, bf16[4096,768]{1,0:T(8,128)(2,1)} %all-gather.4.cloned.1.call-done), kind=kOutput, calls=%fused_computation.34 | convolution fusion | flops 805306368 | bytes 7733248 | tf_op jit(solution)/shard_map/dot_general | solution.py:38
  77.6 58.6 %all-gather.6.cloned.1.call-done = bf16[4096,768]{1,0:T(8,128)(2,1)} async-done(((bf16[256,768]{1,0:T(8,128)(2,1)}), bf16[4096,768]{1,0:T(8,128)(2,1)}) %all-gather.6.cloned.1.call-update) | async-done | bytes 6291472 | tf_op jit(solution)/shard_map/all_gather | solution.py:45
  136.2 62.4 %all-gather.8.cloned.1.call-done = bf16[4096,768]{1,0:T(8,128)(2,1)} async-done(((bf16[256,768]{1,0:T(8,128)(2,1)}), bf16[4096,768]{1,0:T(8,128)(2,1)}) %all-gather.8.cloned.1.call-update) | async-done | bytes 6291472 | tf_op jit(solution)/shard_map/all_gather | solution.py:51
  198.7 9.0 %fusion.1 = f32[128,4096]{1,0:T(8,128)} fusion(bf16[4096,768]{1,0:T(8,128)(2,1)} %all-gather.8.cloned.1.call-done, bf16[128,4096]{1,0:T(8,128)(2,1)S(1)} %convolution_convert_fusion, bf16[4096,768]{1,0:T(8,128)(2,1)} %all-gather.6.cloned.1.call-done, f32[128,768]{1,0:T(8,128)S(1)} %fusion.22), kind=kOutput, calls=%fused_computation.5 | convolution fusion | flops 1611202560 | bytes 16121856 | tf_op jit(solution)/shard_map/dot_general | solution.py:49
  207.7 30.7 %reduce-scatter.2.cloned.1.call-done = f32[128,2048]{1,0:T(8,128)} async-done(((f32[128,4096]{1,0:T(8,128)}), f32[128,2048]{1,0:T(8,128)}) %reduce-scatter.2.cloned.1.call-update) | async-done | bytes 1048592 | tf_op jit(solution)/shard_map/reduce_scatter | solution.py:70
  238.4 9.9 %convolution_convert_fusion.1 = bf16[1024,2048]{1,0:T(8,128)(2,1)} fusion(f32[128,2048]{1,0:T(8,128)} %reduce-scatter.2.cloned.1.call-done, f32[1024]{0:T(1024)S(1)} %get-tuple-element.93, s32[1024]{0:T(1024)S(1)} %get-tuple-element.96, pred[1024]{0:T(1024)(128)(4,1)S(1)} %get-tuple-element.95), kind=kOutput, calls=%fused_computation.2 | convolution fusion | flops 3223715840 | bytes 5252096 | tf_op jit(solution)/shard_map/dot_general | solution.py:71
  (13 shorter events, 0.7 us)
Async XLA Ops:
  6.5 67.3 %all-gather.4.cloned.1.call-start = ((), (), s32[]{:S(2)}) async-start(), calls=%async_computation.1 | async-start | bytes 6684672 | tf_op jit(solution)/shard_map/all_gather | solution.py:40
  7.3 129.0 %all-gather.6.cloned.1.call-start = ((), (), s32[]{:S(2)}) async-start(), calls=%async_computation.2 | async-start | bytes 6684672 | tf_op jit(solution)/shard_map/all_gather | solution.py:45
  8.0 190.6 %all-gather.8.cloned.1.call-start = ((), (), s32[]{:S(2)}) async-start(), calls=%async_computation.3 | async-start | bytes 6684672 | tf_op jit(solution)/shard_map/all_gather | solution.py:51
  8.7 229.7 %reduce-scatter.2.cloned.1.call-start = ((), (), s32[]{:S(2)}) async-start(), calls=%async_computation.4 | async-start | bytes 3145728 | tf_op jit(solution)/shard_map/reduce_scatter | solution.py:70
Sparse Core Ops, SparseCore 0:
  9.6 64.1 all-gather.3
  76.1 60.0 all-gather.5
  138.5 60.0 all-gather.7
  207.8 30.5 reduce-scatter.1
where the time goes:
time: 255 us
  waiting for transfers between devices  177 us (69%)
  matrix products  27.4 us (11%)
  blocking collectives  14.4 us (6%)
  between operations  13.2 us (5%)
  local copies, waits for them, and re-layouts  11.6 us (5%)
  loops' own time  9.59 us (4%)
    all_gather x1, waiting for transfers between devices, run_expert(): lax.all_gather(down_weight, 'wa', axis=0, tiled=True)  62.4 us
    all_gather x1, waiting for transfers between devices, run_expert(): lax.all_gather(up_weight, 'wa', axis=0, tiled=True)  58.6 us
    reduce_scatter x1, waiting for transfers between devices, per_device(): halves = lax.psum_scatter(expert_out, 'ha', scatter_dimension=1, tiled=True)  30.7 us
    all_gather x1, waiting for transfers between devices, run_expert(): lax.all_gather(gate_weight, 'wa', axis=0, tiled=True)  22.8 us
    unnamed x1, blocking collectives  14.4 us
    dot_general x1, matrix products, per_device(): jnp.dot(combine_map, halves, precision=lax.Precision.HIGHEST, preferred_e...  9.87 us
    another operation x1, loops' own time, prefix(): return lax.fori_loop(0, count - 1, turn, subtotal)  9.59 us
    dot_general x1, matrix products, run_expert(): lax.dot_general(hidden, lax.all_gather(down_weight, 'wa', axis=0, tiled=T...  9.02 us
  transfers between devices with their start and end apart: 4, of which 4 were waited for; matrix products, arithmetic and copies ran while one was open for 9% of the time, Pallas kernels for 0%

commit v1 on v0

v1 whole, which is shorter than its diff:
```python
import functools

import jax
import jax.numpy as jnp
from jax import lax
from jax.experimental import pallas as pl
from jax.experimental.pallas import tpu as pltpu
from jax.sharding import PartitionSpec as P

CAP = 128
TOK_COLS = 512
K_BLOCK = 1024
MESH = pl.DeviceIdType.MESH


def expert_kernel(
    n,
    pos_ref, count_ref, tok_ref, gate_ref, up_ref, down_ref,
    y_ref, earlier_ref,
    w, counts, slots, tok_buf, gate_acc, up_acc, hidden, own, sent, got,
    load_sem, tok_sem, c_send, c_recv, r_send, r_recv, d_send, d_recv, o_send, o_recv, x_send, x_recv,
):
    chips = n // 2
    half_ring = chips // 2
    cols = n // 2
    me = lax.axis_index("wa")
    ha = lax.axis_index("ha")
    core = lax.rem(me, 2)
    chip = me // 2
    odd = lax.rem(chip, 2)
    place = (1 - odd) * (chip // 2) + odd * (chips - 1 - chip // 2)

    def at(p):
        p = lax.rem(p + 2 * chips, chips)
        back = p // half_ring
        return 2 * ((1 - back) * 2 * p + back * (2 * (chips - 1 - p) + 1)) + core

    nxt, prv = at(place + 1), at(place - 1)
    sibling = me + 1 - 2 * core

    def origin(direction, step):
        return at(place - step) if direction == 0 else at(place + step)

    def piece(index, k):
        return w.at[k // 2, index, k % 2]

    def ring_send(direction, step, k):
        ref = piece(origin(direction, step - 1), k)
        return pltpu.make_async_remote_copy(
            src_ref=ref, dst_ref=ref,
            send_sem=r_send.at[direction, step - 1, k], recv_sem=r_recv.at[direction, step - 1, k],
            device_id={"wa": nxt if direction == 0 else prv}, device_id_type=MESH,
        )

    def ring_recv(direction, step, k):
        ref = piece(origin(direction, step), k)
        return pltpu.make_async_remote_copy(
            src_ref=ref, dst_ref=ref,
            send_sem=r_send.at[direction, step - 1, k], recv_sem=r_recv.at[direction, step - 1, k],
            device_id={"wa": nxt if direction == 0 else prv}, device_id_type=MESH,
        )

    def pass_on(direction, step, k):
        ref = piece(origin(direction, step), k)
        return pltpu.make_async_remote_copy(
            src_ref=ref, dst_ref=ref,
            send_sem=d_send.at[direction, step - 1, k], recv_sem=d_recv.at[direction, step - 1, k],
            device_id={"wa": sibling}, device_id_type=MESH,
        )

    def other(index):
        return index + 1 - 2 * core

    def passed(direction, step, k):
        ref = piece(other(origin(direction, step)), k)
        return pltpu.make_async_remote_copy(
            src_ref=ref, dst_ref=ref,
            send_sem=d_send.at[direction, step - 1, k], recv_sem=d_recv.at[direction, step - 1, k],
            device_id={"wa": sibling}, device_id_type=MESH,
        )

    def own_pass(t, index):
        return pltpu.make_async_remote_copy(
            src_ref=w.at[t, index], dst_ref=w.at[t, index],
            send_sem=o_send.at[t], recv_sem=o_recv.at[t],
            device_id={"wa": sibling}, device_id_type=MESH,
        )

    def count_copy(k):
        return pltpu.make_async_remote_copy(
            src_ref=count_ref, dst_ref=counts.at[me],
            send_sem=c_send.at[k], recv_sem=c_recv.at[k],
            device_id={"wa": lax.rem(me + k, n)}, device_id_type=MESH,
        )

    def count_got(k):
        return pltpu.make_async_remote_copy(
            src_ref=count_ref, dst_ref=counts.at[lax.rem(me - k + n, n)],
            send_sem=c_send.at[k], recv_sem=c_recv.at[k],
            device_id={"wa": lax.rem(me + k, n)}, device_id_type=MESH,
        )

    def swap(j):
        return pltpu.make_async_remote_copy(
            src_ref=sent.at[j], dst_ref=got.at[j],
            send_sem=x_send.at[j], recv_sem=x_recv.at[j],
            device_id={"ha": 1 - ha}, device_id_type=MESH,
        )

    loads = [
        pltpu.make_async_copy(ref, w.at[t, me], load_sem.at[t])
        for t, ref in enumerate((gate_ref, up_ref, down_ref))
    ]
    for load in loads:
        load.start()
    blocks = tok_ref.shape[1] // TOK_COLS

    def tok_load(i, slot):
        return pltpu.make_async_copy(
            tok_ref.at[:, pl.ds(pl.multiple_of(i * TOK_COLS, TOK_COLS), TOK_COLS)],
            tok_buf.at[slot], tok_sem.at[slot],
        )

    tok_load(0, 0).start()
    tok_load(1, 1).start()

    barrier = pltpu.get_barrier_semaphore()

    @pl.loop(1, n)
    def _(k):
        pl.semaphore_signal(barrier, inc=1, device_id={"wa": lax.rem(me + k, n)}, device_id_type=MESH)

    pl.semaphore_signal(barrier, inc=1, device_id={"ha": 1 - ha}, device_id_type=MESH)
    pl.semaphore_wait(barrier, n)

    for t in range(2):
        loads[t].wait()
        for k in (2 * t, 2 * t + 1):
            for direction in (0, 1):
                ring_send(direction, 1, k).start()
        own_pass(t, me).start()
    loads[2].wait()
    own_pass(2, me).start()

    @pl.loop(1, n)
    def _(k):
        count_copy(k).start()

    slot_ids = lax.broadcasted_iota(jnp.int32, (CAP, pos_ref.shape[1]), 0)
    table = jnp.where(pos_ref[...] == slot_ids, jnp.float32(1.0), jnp.float32(0.0)).astype(jnp.bfloat16)

    @pl.loop(0, blocks)
    def _(i):
        slot = lax.rem(i, 2)
        tok_load(i, slot).wait()
        slots[:, pl.ds(pl.multiple_of(i * TOK_COLS, TOK_COLS), TOK_COLS)] = jnp.dot(
            table, tok_buf[slot], preferred_element_type=jnp.float32
        ).astype(jnp.bfloat16)

        @pl.when(i + 2 < blocks)
        def _():
            tok_load(i + 2, slot).start()

    def serve(step, streams, last_forward):
        for k in streams:
            for direction in (0, 1):
                ring_recv(direction, step, k).wait_recv()
                if not last_forward or k % 2 == direction:
                    ring_send(direction, step + 1, k).start()
                pass_on(direction, step, k).start()

    def serve_end(streams):
        for k in streams:
            direction = k % 2
            ring_recv(direction, half_ring, k).wait_recv()
            pass_on(direction, half_ring, k).start()

    early, late = (0, 1, 2, 3), (4, 5)

    @pl.loop(1, half_ring - 1)
    def _(step):
        serve(step, early, False)

    serve(half_ring - 1, early, True)
    for k in late:
        for direction in (0, 1):
            ring_send(direction, 1, k).start()
    serve_end(early)

    for t in (0, 1):
        own_pass(t, sibling).wait_recv()

    @pl.loop(1, half_ring)
    def _(step):
        for k in early:
            for direction in (0, 1):
                passed(direction, step, k).wait_recv()

    for k in early:
        passed(k % 2, half_ring, k).wait_recv()

    fd = w.shape[2] * w.shape[3]
    per = K_BLOCK // fd
    hid = w.shape[4]
    gate_acc[...] = jnp.zeros_like(gate_acc)
    up_acc[...] = jnp.zeros_like(up_acc)

    @pl.loop(0, n // per)
    def _(i):
        rows = slots[:, pl.ds(pl.multiple_of(i * K_BLOCK, K_BLOCK), K_BLOCK)]
        for t, acc in ((0, gate_acc), (1, up_acc)):
            block = w[t, pl.ds(i * per, per)].reshape(K_BLOCK, hid)
            acc[...] += jnp.dot(rows, block, preferred_element_type=jnp.float32)

    gate = gate_acc[...]
    hidden[...] = (gate / (1.0 + jnp.exp(-gate)) * up_acc[...]).astype(jnp.bfloat16)

    def finish(index):
        part = lax.dot_general(
            hidden[...], w[2, index].reshape(fd, hid), (((1,), (1,)), ((), ())),
            preferred_element_type=jnp.float32,
        )
        j = lax.rem(index, cols)

        @pl.when(index // cols == ha)
        def _():
            own[j] = part

        @pl.when(index // cols != ha)
        def _():
            sent[j] = part.astype(jnp.bfloat16)
            swap(j).start()

    finish(me)
    own_pass(2, sibling).wait_recv()
    finish(sibling)

    def down_step(step):
        for direction in (0, 1):
            index = origin(direction, step)
            finish(index)
            for k in late:
                passed(direction, step, k).wait_recv()
            finish(other(index))

    @pl.loop(1, half_ring - 1)
    def _(step):
        serve(step, late, False)
        down_step(step)

    serve(half_ring - 1, late, True)
    down_step(half_ring - 1)
    serve_end(late)
    far = origin(0, half_ring)
    finish(far)
    for k in late:
        passed(k % 2, half_ring, k).wait_recv()
    finish(other(far))

    @pl.loop(1, n)
    def _(k):
        count_got(k).wait_recv()

    counts[me] = jnp.zeros(counts.shape[1:], jnp.int32)
    total = jnp.zeros(counts.shape[1:], jnp.int32)

    def add_count(i, total):
        return total + jnp.where(i < me, counts[i], 0)

    earlier_ref[...] = lax.fori_loop(0, n, add_count, total)

    for j in range(cols):
        swap(j).wait_recv()
        y = own[j] + got[j].astype(jnp.float32)
        high = y.astype(jnp.bfloat16)
        y_ref[0:CAP, j * fd:(j + 1) * fd] = high
        y_ref[CAP:2 * CAP, j * fd:(j + 1) * fd] = (y - high.astype(jnp.float32)).astype(jnp.bfloat16)

    @pl.loop(1, n)
    def _(k):
        count_copy(k).wait_send()

    for t in range(3):
        own_pass(t, me).wait_send()

    @pl.loop(1, half_ring)
    def _(step):
        for k in range(6):
            for direction in (0, 1):
                ring_send(direction, step, k).wait_send()
                pass_on(direction, step, k).wait_send()

    for k in range(6):
        ring_send(k % 2, half_ring, k).wait_send()
        pass_on(k % 2, half_ring, k).wait_send()

    @pl.loop(0, cols)
    def _(j):
        swap(j).wait_send()


def expert(pos, count, tokens, gate, up, down):
    n = lax.axis_size("wa")
    fd, hid = gate.shape
    half = fd // 2
    steps = n // 4
    cols = n // 2
    any_spec = pl.BlockSpec(memory_space=pl.ANY)
    vmem = pl.BlockSpec(memory_space=pltpu.VMEM)
    dma = pltpu.SemaphoreType.DMA
    return pl.pallas_call(
        functools.partial(expert_kernel, n),
        out_shape=(
            jax.ShapeDtypeStruct((2 * CAP, cols * fd), jnp.bfloat16),
            jax.ShapeDtypeStruct(count.shape, jnp.int32),
        ),
        in_specs=[vmem, vmem, any_spec, any_spec, any_spec, any_spec],
        out_specs=(vmem, vmem),
        scratch_shapes=[
            pltpu.VMEM((3, n, 2, half, hid), jnp.bfloat16),
            pltpu.VMEM((n, *count.shape), jnp.int32),
            pltpu.VMEM((CAP, n * fd), jnp.bfloat16),
            pltpu.VMEM((2, tokens.shape[0], TOK_COLS), jnp.bfloat16),
            pltpu.VMEM((CAP, hid), jnp.float32),
            pltpu.VMEM((CAP, hid), jnp.float32),
            pltpu.VMEM((CAP, hid), jnp.bfloat16),
            pltpu.VMEM((cols, CAP, fd), jnp.float32),
            pltpu.VMEM((cols, CAP, fd), jnp.bfloat16),
            pltpu.VMEM((cols, CAP, fd), jnp.bfloat16),
            dma((3,)), dma((2,)), dma((n,)), dma((n,)),
            dma((2, steps, 6)), dma((2, steps, 6)),
            dma((2, steps, 6)), dma((2, steps, 6)),
            dma((3,)), dma((3,)), dma((cols,)), dma((cols,)),
        ],
        compiler_params=pltpu.CompilerParams(
            collective_id=0, has_side_effects=True, vmem_limit_bytes=60 * 1024 * 1024
        ),
    )(pos, count, tokens, *(v.reshape(2, half, hid) for v in (gate, up, down)))


def per_device(tokens, expert_ids, keep_mask, route_weight, gate_weight, up_weight, down_weight):
    matches = (expert_ids == 0) & (keep_mask == 1)
    chosen = jnp.any(matches, axis=1).astype(jnp.int32)
    route_sum = jnp.sum(jnp.where(matches, route_weight, jnp.float32(0.0)), axis=1)
    position = jnp.cumsum(chosen) - chosen
    place = jnp.where(chosen == 1, position, -1)
    count = jnp.broadcast_to(jnp.sum(chosen), (8, 128))
    y, earlier = expert(place[None, :], count, tokens, gate_weight, up_weight, down_weight)
    capacity = lax.axis_size("wa") * CAP // 2
    slot_ids = lax.rem(jnp.arange(2 * CAP, dtype=jnp.int32), CAP)
    admitted = (place[:, None] == slot_ids[None, :]) & (earlier[0, 0] + place < capacity)[:, None]
    mixed = jnp.dot(admitted.astype(jnp.bfloat16), y, preferred_element_type=jnp.float32)
    return (mixed * route_sum[:, None]).astype(jnp.bfloat16)


def solution(mesh):
    return jax.shard_map(
        per_device,
        mesh=mesh,
        in_specs=(
            P("wa", None),
            P("wa", None),
            P("wa", None),
            P("wa", None),
            P("wa", "ha"),
            P("wa", "ha"),
            P("wa", "ha"),
        ),
        out_specs=P("wa", "ha"),
        check_vma=False,
    )
```

time: 255 us -> 117 us (0.46)
  waiting for transfers between devices: 177 us -> 0 us
  Pallas kernels: 0 us -> 106 us
  matrix products: 27.4 us -> 4.51 us
  blocking collectives: 14.4 us -> 0 us
  between operations: 13.2 us -> 0.02 us
  loops' own time: 9.59 us -> 0 us
  local copies, waits for them, and re-layouts: 11.6 us -> 2.61 us
    all_gather x3 -> x0, waiting for transfers between devices: 144 us -> none  [the longest x1 62.4 us: run_expert(): lax.all_gather(down_weight, 'wa', axis=0, tiled=True)]
    pallas_call x0 -> x1, Pallas kernels: none -> 106 us  [expert(): pl.pallas_call(functools.partial(expert_kernel, n), out_shape=(jax.ShapeD...]
    reduce_scatter x1 -> x0, waiting for transfers between devices: 30.7 us -> none  [per_device(): halves = lax.psum_scatter(expert_out, 'ha', scatter_dimension=1, tiled=True)]
    dot_general x4 -> x1, matrix products: 27.4 us -> 4.51 us  [per_device(): jnp.dot(admitted.astype(jnp.bfloat16), y, preferred_element_type=jnp.floa...]
    unnamed x1 -> x0, blocking collectives: 14.4 us -> none
    another operation x1 -> x0, loops' own time: 9.59 us -> none  [prefix(): return lax.fori_loop(0, count - 1, turn, subtotal)]
    dynamic_slice x15 -> x0, local copies, waits for them, and re-layouts: 8.86 us -> none  [turn(): longer = join(subtotal, pieces[position])]
    unnamed x3 -> x0, local copies, waits for them, and re-layouts: 2.58 us -> none
  transfers between devices with their start and end apart: 4 -> 0, of which waited for: 4 -> 0; matrix products, arithmetic and copies ran while one was open for 9% -> 0% of each run, Pallas kernels for 0% -> 0%
where the time goes in v1:
time: 117 us
  Pallas kernels  106 us (91%)
  matrix products  4.51 us (4%)
  other arithmetic  3.18 us (3%)
  local copies, waits for them, and re-layouts  2.61 us (2%)
    pallas_call x1, Pallas kernels, expert(): pl.pallas_call(functools.partial(expert_kernel, n), out_shape=(jax.ShapeD...  106 us
    dot_general x1, matrix products, per_device(): jnp.dot(admitted.astype(jnp.bfloat16), y, preferred_element_type=jnp.floa...  4.51 us

profile of v1, /device:TPU:0, one launch (start us, length us, event | category | flops | bytes accessed | tf_op | source)
XLA Modules:
  0.0 116.7 jit_solution(5360161642948332423)
XLA Ops:
  0.0 0.8 select_reduce_fusion
  0.8 0.6 convert_reduce_fusion
  1.5 1.2 %broadcast_in_dim.20.count_ref = s32[8,128]{1,0:T(8,128)} broadcast(s32[]{:T(128)} %convert_reduce_fusion), dimensions={} | broadcast | bytes 4100 | tf_op jit(solution)/shard_map/broadcast_in_dim | solution.py:347
  2.7 0.3 reduce-window.9
  3.0 0.1 slice.10
  3.1 0.1 slice_reduce_fusion
  3.2 0.1 broadcast_add_fusion
  3.3 0.6 compare_select_fusion.pos_ref
  3.9 106.4 %shard_map.73 = (bf16[256,2048]{1,0:T(8,128)(2,1)}, s32[8,128]{1,0:T(8,128)}) custom-call(s32[1,1024]{1,0:T(1,128)} %compare_select_fusion.pos_ref, s32[8,128]{1,0:T(8,128)} %broadcast_in_dim.20.count_ref, bf16[1024,4096]{1,0:T(8,128)(2,1)} %tok_ref.1, bf16[2,128,768]{2,1,0:T(8,128)(2,1)} %bitcast.12, bf16[2,128,768]{2,1,0:T(8,128)(2,1)} %bitcast.13, ...), custom_call_target="tpu_custom_call" | custom-call | tf_op jit(solution)/shard_map/pallas_call | solution.py:311
  110.3 1.2 %slice.12 = s32[1,1]{1,0:T(1,128)} slice(s32[8,128]{1,0:T(8,128)} %get-tuple-element.7), slice={[0:1], [0:1]} | slice | bytes 8 | tf_op jit(solution)/shard_map/slice | solution.py:351
  111.5 0.7 add_compare_fusion
  112.2 4.5 %multiply_convert_fusion = bf16[1024,2048]{1,0:T(8,128)(2,1)} fusion(bf16[256,2048]{1,0:T(8,128)(2,1)} %get-tuple-element.8, f32[1024]{0:T(1024)S(1)} %get-tuple-element.11, s32[256]{0:T(256)S(1)} %iota_and_fusion, s32[1024]{0:T(1024)S(1)} %get-tuple-element.10, pred[1024]{0:T(1024)(128)(4,1)S(1)} %get-tuple-element.9), kind=kOutput, calls=%fused_computation | convolution fusion | flops 1078460416 | bytes 5253120 | tf_op jit(solution)/shard_map/dot_general | solution.py:352
  (4 shorter events, 0.1 us)

commit v2 on v0

v2 whole, which is shorter than its diff:
```python
import functools

import jax
import jax.numpy as jnp
from jax import lax
from jax.experimental import pallas as pl
from jax.experimental.pallas import tpu as pltpu
from jax.sharding import PartitionSpec as P

CAP = 128
TOK_COLS = 512
MESH = pl.DeviceIdType.MESH


def expert_kernel(
    n,
    pos_ref, tok_ref, gate_ref, up_ref, down_ref,
    y_ref,
    w, wd, count, counts, slots, guest, tok_buf, part_out, part_in, gate_acc, up_acc, hidden, own, sent, got,
    load_sem, tok_sem, c_send, c_recv, r_send, r_recv, d_send, d_recv, rd_send, rd_recv, dd_send, dd_recv,
    o_send, o_recv, g_send, g_recv, h_send, h_recv, p_send, p_recv, x_send, x_recv,
):
    side = n // 2
    me = lax.axis_index("wa")
    ha = lax.axis_index("ha")
    core = lax.rem(me, 2)
    half = me // side
    sibling = me + 1 - 2 * core
    across = lax.rem(me + side, n)

    def remote(ref, dst, send, recv, **where):
        return pltpu.make_async_remote_copy(
            src_ref=ref, dst_ref=dst, send_sem=send, recv_sem=recv, device_id=where, device_id_type=MESH
        )

    class Ring:
        def __init__(self, members, base, ref_of, sems):
            self.chips, self.base, self.ref_of = members // 2, base, ref_of
            self.steps = self.chips // 2
            self.r_send, self.r_recv, self.d_send, self.d_recv = sems
            chip = (me - base) // 2
            odd = lax.rem(chip, 2)
            self.place = (1 - odd) * (chip // 2) + odd * (self.chips - 1 - chip // 2)
            self.to = (base + self.at(self.place + 1), base + self.at(self.place - 1))

        def at(self, p):
            p = lax.rem(p + 2 * self.chips, self.chips)
            back = p // self.steps
            return 2 * ((1 - back) * 2 * p + back * (2 * (self.chips - 1 - p) + 1)) + core

        def origin(self, direction, step):
            return self.at(self.place - step) if direction == 0 else self.at(self.place + step)

        def _hop(self, ref, direction, step, k):
            return remote(
                ref, ref, self.r_send.at[direction, step - 1, k], self.r_recv.at[direction, step - 1, k],
                wa=self.to[direction],
            )

        def _pass(self, ref, direction, step, k):
            return remote(
                ref, ref, self.d_send.at[direction, step - 1, k], self.d_recv.at[direction, step - 1, k], wa=sibling
            )

        def send(self, direction, step, k):
            return self._hop(self.ref_of(self.origin(direction, step - 1), k), direction, step, k)

        def recv(self, direction, step, k):
            return self._hop(self.ref_of(self.origin(direction, step), k), direction, step, k)

        def pass_on(self, direction, step, k):
            return self._pass(self.ref_of(self.origin(direction, step), k), direction, step, k)

        def passed(self, direction, step, k):
            index = self.origin(direction, step) + 1 - 2 * core
            return self._pass(self.ref_of(index, k), direction, step, k)

        def serve(self, step, streams, last_forward):
            for k in streams:
                for direction in (0, 1):
                    self.recv(direction, step, k).wait_recv()
                    if not last_forward or k % 2 == direction:
                        self.send(direction, step + 1, k).start()
                    self.pass_on(direction, step, k).start()

        def serve_end(self, streams):
            for k in streams:
                self.recv(k % 2, self.steps, k).wait_recv()
                self.pass_on(k % 2, self.steps, k).start()

        def drain(self, streams):
            @pl.loop(1, self.steps)
            def _(step):
                for k in streams:
                    for direction in (0, 1):
                        self.send(direction, step, k).wait_send()
                        self.pass_on(direction, step, k).wait_send()

            for k in streams:
                self.send(k % 2, self.steps, k).wait_send()
                self.pass_on(k % 2, self.steps, k).wait_send()

    near = Ring(side, half * side, lambda i, k: w.at[k // 2, i, k % 2], (r_send, r_recv, d_send, d_recv))
    full = Ring(n, 0, lambda i, k: wd.at[i, k], (rd_send, rd_recv, dd_send, dd_recv))
    mine = me - half * side
    early, late = (0, 1, 2, 3), (0, 1)

    def own_pass(t, index):
        ref = wd.at[index] if t == 2 else w.at[t, index - half * side]
        return remote(ref, ref, o_send.at[t], o_recv.at[t], wa=sibling)

    def count_copy(k):
        return remote(count, counts.at[me], c_send.at[k], c_recv.at[k], wa=lax.rem(me + k, n))

    def count_got(k):
        return remote(count, counts.at[lax.rem(me - k + n, n)], c_send.at[k], c_recv.at[k], wa=lax.rem(me + k, n))

    def swap(j):
        return remote(sent.at[j], got.at[j], x_send.at[j], x_recv.at[j], ha=1 - ha)

    loads = [
        pltpu.make_async_copy(gate_ref, w.at[0, mine], load_sem.at[0]),
        pltpu.make_async_copy(up_ref, w.at[1, mine], load_sem.at[1]),
        pltpu.make_async_copy(down_ref, wd.at[me], load_sem.at[2]),
    ]
    for load in loads:
        load.start()
    quarter = slots.shape[2]
    per_quarter = quarter // TOK_COLS
    leaving = 2 * (1 - half) + ha
    wanted = (leaving, 2 * half, 2 * half + 1)
    blocks = len(wanted) * per_quarter

    def tok_load(i):
        start = wanted[i // per_quarter] * quarter + i % per_quarter * TOK_COLS
        return pltpu.make_async_copy(
            tok_ref.at[:, pl.ds(pl.multiple_of(start, TOK_COLS), TOK_COLS)], tok_buf.at[i % 2], tok_sem.at[i % 2]
        )

    tok_load(0).start()
    tok_load(1).start()
    place = pos_ref[...]
    chosen = jnp.sum(jnp.where(place >= 0, 1, 0), axis=1, keepdims=True)
    count[...] = jnp.broadcast_to(chosen, count.shape)

    barrier = pltpu.get_barrier_semaphore()

    @pl.loop(1, n)
    def _(k):
        pl.semaphore_signal(barrier, inc=1, device_id={"wa": lax.rem(me + k, n)}, device_id_type=MESH)

    pl.semaphore_signal(barrier, inc=1, device_id={"ha": 1 - ha}, device_id_type=MESH)
    pl.semaphore_wait(barrier, n)

    for t in range(2):
        loads[t].wait()
        for k in (2 * t, 2 * t + 1):
            for direction in (0, 1):
                near.send(direction, 1, k).start()
        own_pass(t, me).start()
    loads[2].wait()
    own_pass(2, me).start()

    slot_ids = lax.broadcasted_iota(jnp.int32, (CAP, pos_ref.shape[1]), 0)
    table = jnp.where(place == slot_ids, jnp.float32(1.0), jnp.float32(0.0)).astype(jnp.bfloat16)
    guest_out = remote(slots.at[0], guest.at[ha], g_send, g_recv, wa=across)
    guest_in = guest_out
    share = remote(guest.at[ha], guest.at[ha], h_send, h_recv, ha=1 - ha)
    shared = remote(guest.at[1 - ha], guest.at[1 - ha], h_send, h_recv, ha=1 - ha)
    for i in range(blocks):
        tok_load(i).wait()
        slots[i // per_quarter, :, i % per_quarter * TOK_COLS:(i % per_quarter + 1) * TOK_COLS] = jnp.dot(
            table, tok_buf[i % 2], preferred_element_type=jnp.float32
        ).astype(jnp.bfloat16)
        if i + 2 < blocks:
            tok_load(i + 2).start()
        if i == per_quarter:
            guest_out.start()

    @pl.loop(1, n)
    def _(k):
        count_copy(k).start()

    @pl.loop(1, near.steps - 1)
    def _(step):
        near.serve(step, early, False)

    near.serve(near.steps - 1, early, True)
    guest_in.wait_recv()
    share.start()
    for k in late:
        for direction in (0, 1):
            full.send(direction, 1, k).start()
    near.serve_end(early)
    for t in (0, 1):
        own_pass(t, sibling).wait_recv()

    @pl.loop(1, near.steps)
    def _(step):
        for k in early:
            for direction in (0, 1):
                near.passed(direction, step, k).wait_recv()

    for k in early:
        near.passed(k % 2, near.steps, k).wait_recv()
    shared.wait_recv()

    hid = w.shape[4]
    group = side // 2

    def project(rows, t):
        total = None
        for q in (0, 1):
            block = w[t, q * group:(q + 1) * group].reshape(quarter, hid)
            term = jnp.dot(rows[q], block, preferred_element_type=jnp.float32)
            total = term if total is None else total + term
        return total

    def partial(t):
        return remote(part_out.at[t], part_in.at[t], p_send.at[t], p_recv.at[t], wa=across)

    part_out[0] = project((guest[0], guest[1]), 0).astype(jnp.bfloat16)
    part_out[1] = project((guest[0], guest[1]), 1).astype(jnp.bfloat16)
    partial(0).start()
    partial(1).start()
    gate_acc[...] = project((slots[1], slots[2]), 0)
    up_acc[...] = project((slots[1], slots[2]), 1)

    ahead = full.steps // 2

    @pl.loop(1, ahead + 1)
    def _(step):
        full.serve(step, late, False)

    partial(0).wait_recv()
    partial(1).wait_recv()
    gate = gate_acc[...] + part_in[0].astype(jnp.float32)
    up = up_acc[...] + part_in[1].astype(jnp.float32)
    hidden[...] = (gate / (1.0 + jnp.exp(-gate)) * up).astype(jnp.bfloat16)
    fd = wd.shape[1] * wd.shape[2]

    def finish(index):
        part = lax.dot_general(
            hidden[...], wd[index].reshape(fd, hid), (((1,), (1,)), ((), ())),
            preferred_element_type=jnp.float32,
        )
        j = lax.rem(index, side)

        @pl.when(index // side == ha)
        def _():
            own[j] = part

        @pl.when(index // side != ha)
        def _():
            sent[j] = part.astype(jnp.bfloat16)
            swap(j).start()

    finish(me)
    own_pass(2, sibling).wait_recv()
    finish(sibling)

    def down_step(step):
        for direction in (0, 1):
            index = full.origin(direction, step)
            finish(index)
            for k in late:
                full.passed(direction, step, k).wait_recv()
            finish(index + 1 - 2 * core)

    @pl.loop(1, ahead + 1)
    def _(step):
        down_step(step)

    @pl.loop(ahead + 1, full.steps - 1)
    def _(step):
        full.serve(step, late, False)
        down_step(step)

    full.serve(full.steps - 1, late, True)
    down_step(full.steps - 1)
    full.serve_end(late)
    far = full.origin(0, full.steps)
    finish(far)
    for k in late:
        full.passed(k % 2, full.steps, k).wait_recv()
    finish(far + 1 - 2 * core)

    @pl.loop(1, n)
    def _(k):
        count_got(k).wait_recv()

    counts[me] = jnp.zeros(counts.shape[1:], jnp.int32)

    def add_count(i, total):
        return total + jnp.where(i < me, counts[i], 0)

    earlier = lax.fori_loop(0, n, add_count, jnp.zeros(counts.shape[1:], jnp.int32))
    slot = lax.broadcasted_iota(jnp.int32, (CAP, fd), 0)
    admitted = slot + earlier[0:1, 0:1] < side * CAP

    for j in range(side):
        swap(j).wait_recv()
        y = jnp.where(admitted, own[j] + got[j].astype(jnp.float32), jnp.float32(0.0))
        high = y.astype(jnp.bfloat16)
        y_ref[0:CAP, j * fd:(j + 1) * fd] = high
        y_ref[CAP:2 * CAP, j * fd:(j + 1) * fd] = (y - high.astype(jnp.float32)).astype(jnp.bfloat16)

    @pl.loop(1, n)
    def _(k):
        count_copy(k).wait_send()

    for t in range(3):
        own_pass(t, me).wait_send()
    guest_out.wait_send()
    share.wait_send()
    partial(0).wait_send()
    partial(1).wait_send()
    near.drain(early)
    full.drain(late)

    @pl.loop(0, side)
    def _(j):
        swap(j).wait_send()


def expert(pos, tokens, gate, up, down):
    n = lax.axis_size("wa")
    fd, hid = gate.shape
    half = fd // 2
    side = n // 2
    quarter = tokens.shape[1] // 4
    any_spec = pl.BlockSpec(memory_space=pl.ANY)
    vmem = pl.BlockSpec(memory_space=pltpu.VMEM)
    dma = pltpu.SemaphoreType.DMA
    return pl.pallas_call(
        functools.partial(expert_kernel, n),
        out_shape=jax.ShapeDtypeStruct((2 * CAP, side * fd), jnp.bfloat16),
        in_specs=[vmem, any_spec, any_spec, any_spec, any_spec],
        out_specs=vmem,
        scratch_shapes=[
            pltpu.VMEM((2, side, 2, half, hid), jnp.bfloat16),
            pltpu.VMEM((n, 2, half, hid), jnp.bfloat16),
            pltpu.VMEM((8, 128), jnp.int32),
            pltpu.VMEM((n, 8, 128), jnp.int32),
            pltpu.VMEM((3, CAP, quarter), jnp.bfloat16),
            pltpu.VMEM((2, CAP, quarter), jnp.bfloat16),
            pltpu.VMEM((2, tokens.shape[0], TOK_COLS), jnp.bfloat16),
            pltpu.VMEM((2, CAP, hid), jnp.bfloat16),
            pltpu.VMEM((2, CAP, hid), jnp.bfloat16),
            pltpu.VMEM((CAP, hid), jnp.float32),
            pltpu.VMEM((CAP, hid), jnp.float32),
            pltpu.VMEM((CAP, hid), jnp.bfloat16),
            pltpu.VMEM((side, CAP, fd), jnp.float32),
            pltpu.VMEM((side, CAP, fd), jnp.bfloat16),
            pltpu.VMEM((side, CAP, fd), jnp.bfloat16),
            dma((3,)), dma((2,)), dma((n,)), dma((n,)),
            *[dma((2, n // 8, 4)) for _ in range(4)],
            *[dma((2, n // 4, 2)) for _ in range(4)],
            dma((3,)), dma((3,)), dma, dma, dma, dma, dma((2,)), dma((2,)), dma((side,)), dma((side,)),
        ],
        compiler_params=pltpu.CompilerParams(
            collective_id=0, has_side_effects=True, vmem_limit_bytes=60 * 1024 * 1024
        ),
    )(pos, tokens, *(v.reshape(2, half, hid) for v in (gate, up, down)))


def per_device(tokens, expert_ids, keep_mask, route_weight, gate_weight, up_weight, down_weight):
    matches = (expert_ids == 0) & (keep_mask == 1)
    chosen = jnp.any(matches, axis=1).astype(jnp.int32)
    route_sum = jnp.sum(jnp.where(matches, route_weight, jnp.float32(0.0)), axis=1)
    position = jnp.cumsum(chosen) - chosen
    place = jnp.where(chosen == 1, position, -1)
    y = expert(place[None, :], tokens, gate_weight, up_weight, down_weight)
    slot_ids = lax.rem(jnp.arange(2 * CAP, dtype=jnp.int32), CAP)
    combine = (place[:, None] == slot_ids[None, :]).astype(jnp.bfloat16)
    mixed = jnp.dot(combine, y, preferred_element_type=jnp.float32)
    return (mixed * route_sum[:, None]).astype(jnp.bfloat16)


def solution(mesh):
    return jax.shard_map(
        per_device,
        mesh=mesh,
        in_specs=(
            P("wa", None),
            P("wa", None),
            P("wa", None),
            P("wa", None),
            P("wa", "ha"),
            P("wa", "ha"),
            P("wa", "ha"),
        ),
        out_specs=P("wa", "ha"),
        check_vma=False,
    )
```

time: 255 us -> 96.7 us (0.38)
  waiting for transfers between devices: 177 us -> 0 us
  Pallas kernels: 0 us -> 89.7 us
  matrix products: 27.4 us -> 4.45 us
  blocking collectives: 14.4 us -> 0 us
  between operations: 13.2 us -> 0.02 us
  local copies, waits for them, and re-layouts: 11.6 us -> 0.19 us
  loops' own time: 9.59 us -> 0 us
    all_gather x3 -> x0, waiting for transfers between devices: 144 us -> none  [the longest x1 62.4 us: run_expert(): lax.all_gather(down_weight, 'wa', axis=0, tiled=True)]
    pallas_call x0 -> x1, Pallas kernels: none -> 89.7 us  [expert(): pl.pallas_call(functools.partial(expert_kernel, n), out_shape=jax.ShapeDt...]
    reduce_scatter x1 -> x0, waiting for transfers between devices: 30.7 us -> none  [per_device(): halves = lax.psum_scatter(expert_out, 'ha', scatter_dimension=1, tiled=True)]
    dot_general x4 -> x1, matrix products: 27.4 us -> 4.45 us  [per_device(): mixed = jnp.dot(combine, y, preferred_element_type=jnp.float32)]
    unnamed x1 -> x0, blocking collectives: 14.4 us -> none
    another operation x1 -> x0, loops' own time: 9.59 us -> none  [prefix(): return lax.fori_loop(0, count - 1, turn, subtotal)]
    dynamic_slice x15 -> x0, local copies, waits for them, and re-layouts: 8.86 us -> none  [turn(): longer = join(subtotal, pieces[position])]
    unnamed x3 -> x0, local copies, waits for them, and re-layouts: 2.58 us -> none
  transfers between devices with their start and end apart: 4 -> 0, of which waited for: 4 -> 0; matrix products, arithmetic and copies ran while one was open for 9% -> 0% of each run, Pallas kernels for 0% -> 0%
where the time goes in v2:
time: 96.7 us; the launch traced here: 96.2 us
  Pallas kernels  89.7 us (93%)
  matrix products  4.45 us (5%)
  other arithmetic  1.83 us (2%)
    pallas_call x1, Pallas kernels, expert(): pl.pallas_call(functools.partial(expert_kernel, n), out_shape=jax.ShapeDt...  89.7 us
    dot_general x1, matrix products, per_device(): mixed = jnp.dot(combine, y, preferred_element_type=jnp.float32)  4.45 us

profile of v2, /device:TPU:0, one launch (start us, length us, event | category | flops | bytes accessed | tf_op | source)
XLA Modules:
  0.0 96.2 jit_solution(10847864239483844496)
XLA Ops:
  0.0 0.8 select_reduce_fusion
  0.9 0.3 reduce-window.9
  1.1 0.1 slice.7
  1.2 0.1 slice_reduce_fusion
  1.4 0.1 fusion.3
  1.4 0.6 compare_select_fusion.pos_ref
  2.0 89.7 %shard_map.73 = bf16[256,2048]{1,0:T(8,128)(2,1)} custom-call(s32[1,1024]{1,0:T(1,128)} %compare_select_fusion.pos_ref, bf16[1024,4096]{1,0:T(8,128)(2,1)} %tok_ref.1, bf16[2,128,768]{2,1,0:T(8,128)(2,1)} %bitcast.10, bf16[2,128,768]{2,1,0:T(8,128)(2,1)} %bitcast.11, bf16[2,128,768]{2,1,0:T(8,128)(2,1)} %bitcast.12), custom_call_target="tpu_custom_call" | custom-call | tf_op jit(solution)/shard_map/pallas_call | solution.py:335
  91.8 4.4 %multiply_convert_fusion = bf16[1024,2048]{1,0:T(8,128)(2,1)} fusion(bf16[256,2048]{1,0:T(8,128)(2,1)} %shard_map.73, f32[1024]{0:T(1024)S(1)} %get-tuple-element.7, s32[256]{0:T(256)S(1)} %iota_and_fusion, s32[1024]{0:T(1024)S(1)} %get-tuple-element.5), kind=kOutput, calls=%fused_computation | convolution fusion | flops 1078198272 | bytes 5252096 | tf_op jit(solution)/shard_map/dot_general | solution.py:376
  (4 shorter events, 0.1 us)

commit v3 on v2

--- a/solution.py
+++ b/solution.py
@@ -191,20 +191,6 @@
     for k in late:
         for direction in (0, 1):
             full.send(direction, 1, k).start()
-    near.serve_end(early)
-    for t in (0, 1):
-        own_pass(t, sibling).wait_recv()
-
-    @pl.loop(1, near.steps)
-    def _(step):
-        for k in early:
-            for direction in (0, 1):
-                near.passed(direction, step, k).wait_recv()
-
-    for k in early:
-        near.passed(k % 2, near.steps, k).wait_recv()
-    shared.wait_recv()
-
     hid = w.shape[4]
     group = side // 2
 
@@ -219,19 +205,35 @@
     def partial(t):
         return remote(part_out.at[t], part_in.at[t], p_send.at[t], p_recv.at[t], wa=across)
 
+    def gathered(t):
+        streams = (2 * t, 2 * t + 1)
+        near.serve_end(streams)
+        own_pass(t, sibling).wait_recv()
+
+        @pl.loop(1, near.steps)
+        def _(step):
+            for k in streams:
+                for direction in (0, 1):
+                    near.passed(direction, step, k).wait_recv()
+
+        for k in streams:
+            near.passed(k % 2, near.steps, k).wait_recv()
+
+    gathered(0)
+    shared.wait_recv()
     part_out[0] = project((guest[0], guest[1]), 0).astype(jnp.bfloat16)
+    gate_acc[...] = project((slots[1], slots[2]), 0)
+    partial(0).start()
+    gathered(1)
     part_out[1] = project((guest[0], guest[1]), 1).astype(jnp.bfloat16)
-    partial(0).start()
     partial(1).start()
-    gate_acc[...] = project((slots[1], slots[2]), 0)
     up_acc[...] = project((slots[1], slots[2]), 1)
 
-    ahead = full.steps // 2
-
-    @pl.loop(1, ahead + 1)
+    @pl.loop(1, full.steps - 1)
     def _(step):
         full.serve(step, late, False)
 
+    full.serve(full.steps - 1, late, True)
     partial(0).wait_recv()
     partial(1).wait_recv()
     gate = gate_acc[...] + part_in[0].astype(jnp.float32)
@@ -267,18 +269,12 @@
                 full.passed(direction, step, k).wait_recv()
             finish(index + 1 - 2 * core)
 
-    @pl.loop(1, ahead + 1)
+    @pl.loop(1, full.steps - 1)
     def _(step):
         down_step(step)
 
-    @pl.loop(ahead + 1, full.steps - 1)
-    def _(step):
-        full.serve(step, late, False)
-        down_step(step)
-
-    full.serve(full.steps - 1, late, True)
+    full.serve_end(late)
     down_step(full.steps - 1)
-    full.serve_end(late)
     far = full.origin(0, full.steps)
     finish(far)
     for k in late:

time: 96.7 us -> 97.8 us (1.011)
  Pallas kernels: 89.7 us -> 91 us
    pallas_call x1, Pallas kernels: 89.7 us -> 91 us  [expert(): pl.pallas_call(functools.partial(expert_kernel, n), out_shape=jax.ShapeDt...]
where the time goes in v3:
time: 97.8 us; the launch traced here: 97.5 us
  Pallas kernels  91 us (93%)
  matrix products  4.45 us (5%)
  other arithmetic  1.83 us (2%)
    pallas_call x1, Pallas kernels, expert(): pl.pallas_call(functools.partial(expert_kernel, n), out_shape=jax.ShapeDt...  91 us
    dot_general x1, matrix products, per_device(): mixed = jnp.dot(combine, y, preferred_element_type=jnp.float32)  4.45 us

profile of v3, /device:TPU:0, one launch (start us, length us, event | category | flops | bytes accessed | tf_op | source)
XLA Modules:
  0.0 97.5 jit_solution(13465240145941830823)
XLA Ops:
  0.0 0.8 select_reduce_fusion
  0.9 0.3 reduce-window.9
  1.1 0.1 slice.7
  1.2 0.1 slice_reduce_fusion
  1.4 0.1 fusion.3
  1.4 0.6 compare_select_fusion.pos_ref
  2.0 91.0 %shard_map.73 = bf16[256,2048]{1,0:T(8,128)(2,1)} custom-call(s32[1,1024]{1,0:T(1,128)} %compare_select_fusion.pos_ref, bf16[1024,4096]{1,0:T(8,128)(2,1)} %tok_ref.1, bf16[2,128,768]{2,1,0:T(8,128)(2,1)} %bitcast.10, bf16[2,128,768]{2,1,0:T(8,128)(2,1)} %bitcast.11, bf16[2,128,768]{2,1,0:T(8,128)(2,1)} %bitcast.12), custom_call_target="tpu_custom_call" | custom-call | tf_op jit(solution)/shard_map/pallas_call | solution.py:331
  93.0 4.4 %multiply_convert_fusion = bf16[1024,2048]{1,0:T(8,128)(2,1)} fusion(bf16[256,2048]{1,0:T(8,128)(2,1)} %shard_map.73, f32[1024]{0:T(1024)S(1)} %get-tuple-element.7, s32[256]{0:T(256)S(1)} %iota_and_fusion, s32[1024]{0:T(1024)S(1)} %get-tuple-element.5), kind=kOutput, calls=%fused_computation | convolution fusion | flops 1078198272 | bytes 5252096 | tf_op jit(solution)/shard_map/dot_general | solution.py:372
  (4 shorter events, 0.1 us)
